TPU v7x, 768 devices: a whole 4x8x12 slice. The times are simulated.
768 devices in a mesh: row: 96 (over z, y), col: 8 (over x, core).
Axes of the slice: x: 4, y: 8, z: 12, core: 2. Of those that a mesh axis runs over, the one named last changes fastest.
Arguments:
- concentration: float32 [96, 96, 768], P('row', 'col'), may hold values from -2.5 to 2.5
- plane_counts: int32 [8], replicated, may hold values from 1 to 73, 385 in all
Outputs:
- new_concentration: float32 [96, 96, 768], P('row', 'col')
- chemical_potential: float32 [96, 96, 768], P('row', 'col')
- plane_power: float32 [584], P('col')
Inputs may be any that keep to these rules, and one draw needn't show every extreme that they name: Column device j owns the x wavenumber planes o_j to o_j + plane_counts[j] - 1, with o_j the sum of the counts before it; the counts sum to 385 and the largest is exactly 73.
All inputs are finite; a program needn't handle non-finite values.
Results may differ from a plain program's by a relative error of at most 0.000096.
Values sent between devices are 32-bit elements; how exact they have to be, the bound alone decides.
A program may use at most 32 MiB of HBM per device.

v0:
```python
import math

import jax
import jax.numpy as jnp
from jax import lax
from jax.sharding import Mesh
from jax.sharding import PartitionSpec as P

COL = ("col_0", "col_1")
ROW = ("row_0", "row_1")
ROW_COL = ("row_0", "row_1", "col_0", "col_1")


time_step = 16.0
grad_coeff = 1.0
power_floor = 1e-06
highest = lax.Precision.HIGHEST


def one_axis_at_a_time(shard, axes):
    for axis in axes:
        shard = lax.psum(shard, axis)
    return shard


def circle(points):
    positions = jnp.arange(points, dtype=jnp.int32)
    winding = positions[:, None] * positions[None, :] % points
    phases = winding.astype(jnp.float32) * (2.0 * math.pi / points)
    return (jnp.cos(phases), jnp.sin(phases))


def magnitude(positions, points):
    folded = jnp.minimum(positions, points - positions).astype(jnp.float32)
    return folded * (2.0 * math.pi / points)


def rotate(real_part, imag_part, cosine_table, sine_table, orientation, pattern):
    cos_real = jnp.einsum(pattern, cosine_table, real_part, precision=highest)
    cos_imag = jnp.einsum(pattern, cosine_table, imag_part, precision=highest)
    sin_real = jnp.einsum(pattern, sine_table, real_part, precision=highest)
    sin_imag = jnp.einsum(pattern, sine_table, imag_part, precision=highest)
    return jnp.stack([cos_real - orientation * sin_imag, cos_imag + orientation * sin_real], axis=3)


def shards(concentration, plane_counts):
    z_cells, y_cells, x_cells = concentration.shape
    columns = lax.axis_size(COL)
    row_count = lax.axis_size(ROW)
    y_total = y_cells * columns
    z_total = z_cells * row_count
    ky_cells = y_total // row_count
    planes = x_cells // 2 + 1
    even_share = (planes + columns - 1) // columns
    owned_slots = 3 * even_share // 2
    col_index = lax.axis_index(COL)
    row_index = lax.axis_index(ROW)
    owned_starts = jnp.cumsum(plane_counts) - plane_counts
    starts = jnp.arange(columns, dtype=jnp.int32) * even_share
    plane_sizes = jnp.clip(planes - starts, 0, even_share)
    slot_ids = jnp.arange(even_share, dtype=jnp.int32)
    plane_ids = starts[:, None] + slot_ids[None, :]
    in_use = (slot_ids[None, :] < plane_sizes[:, None]).astype(jnp.float32)
    x_index = jnp.arange(x_cells, dtype=jnp.int32)
    winding = x_index[:, None, None] * plane_ids[None, :, :] % x_cells
    phases = winding.astype(jnp.float32) * (2.0 * math.pi / x_cells)
    forward_table = jnp.stack(
        [jnp.cos(phases) * in_use, -jnp.sin(phases) * in_use], axis=1
    ).reshape(x_cells, -1)
    nonlinear = concentration * concentration * concentration - concentration
    fields = jnp.stack([concentration, nonlinear]).reshape(2 * z_cells * y_cells, x_cells)
    spectra = jnp.dot(fields, forward_table, precision=highest, preferred_element_type=jnp.float32)
    spectra = spectra.reshape(2, z_cells, y_cells, 2, columns, even_share)
    spectra = lax.all_to_all(spectra, COL, split_axis=4, concat_axis=2, tiled=True)
    spectra = spectra.reshape(2, z_cells, y_total, 2, even_share)
    y_cosine, y_sine = circle(y_total)
    spectra = rotate(
        spectra[:, :, :, 0], spectra[:, :, :, 1], y_cosine, y_sine, -1.0, "ky,fdys->fdks"
    )
    spectra = lax.all_to_all(spectra, ROW, split_axis=2, concat_axis=1, tiled=True)
    z_cosine, z_sine = circle(z_total)
    spectra = rotate(
        spectra[:, :, :, 0], spectra[:, :, :, 1], z_cosine, z_sine, -1.0, "kz,fzys->fkys"
    )
    my_planes = lax.dynamic_index_in_dim(plane_ids, col_index, 0, keepdims=False)
    x_waves = my_planes.astype(jnp.float32) * (2.0 * math.pi / x_cells)
    y_waves = magnitude(row_index * ky_cells + jnp.arange(ky_cells, dtype=jnp.int32), y_total)
    z_waves = magnitude(jnp.arange(z_total, dtype=jnp.int32), z_total)
    squared = (
        z_waves[:, None, None] ** 2 + y_waves[None, :, None] ** 2 + x_waves[None, None, :] ** 2
    )
    damping = 1.0 + time_step * grad_coeff * squared * squared
    new_real = (spectra[0, :, :, 0] - time_step * squared * spectra[1, :, :, 0]) / damping
    new_imag = (spectra[0, :, :, 1] - time_step * squared * spectra[1, :, :, 1]) / damping
    chem_real = spectra[1, :, :, 0] + grad_coeff * squared * new_real
    chem_imag = spectra[1, :, :, 1] + grad_coeff * squared * new_imag
    partial_power = jnp.sum(new_real * new_real + new_imag * new_imag, axis=(0, 1))
    power_scale = 1.0 / float(x_cells * y_total * y_total * z_total * z_total)
    count_mine = plane_counts[col_index]
    start_mine = owned_starts[col_index]
    owned_ids = jnp.arange(owned_slots, dtype=jnp.int32)
    owned_use = owned_ids < count_mine
    selector = (jnp.arange(columns, dtype=jnp.int32) == col_index).astype(jnp.float32)
    spread = (selector[:, None] * partial_power[None, :]).reshape(-1)
    summed = one_axis_at_a_time(spread, ROW_COL)
    padded = jnp.concatenate([summed, jnp.zeros((owned_slots,), jnp.float32)])
    picked = lax.dynamic_slice_in_dim(padded, start_mine, owned_slots)
    log_power = jnp.where(owned_use, jnp.log(picked * power_scale + power_floor), 0.0)
    new_fields = rotate(
        jnp.stack([new_real, chem_real]),
        jnp.stack([new_imag, chem_imag]),
        z_cosine,
        z_sine,
        1.0,
        "kz,fzys->fkys",
    )
    new_fields = lax.all_to_all(new_fields, ROW, split_axis=1, concat_axis=2, tiled=True)
    new_fields = rotate(
        new_fields[:, :, :, 0], new_fields[:, :, :, 1], y_cosine, y_sine, 1.0, "ky,fdys->fdks"
    )
    new_fields = new_fields.reshape(2, z_cells, y_total, 2, 1, even_share)
    new_fields = lax.all_to_all(new_fields, COL, split_axis=2, concat_axis=4, tiled=True)
    edge_plane = (plane_ids == 0) | (2 * plane_ids == x_cells)
    weights = jnp.where(edge_plane, 1.0, 2.0) * in_use / float(x_cells * y_total * z_total)
    inverse_table = jnp.stack(
        [jnp.cos(phases) * weights, -jnp.sin(phases) * weights], axis=1
    ).reshape(x_cells, -1)
    result = lax.dot_general(
        new_fields.reshape(2 * z_cells * y_cells, -1),
        inverse_table,
        (((1,), (1,)), ((), ())),
        precision=highest,
        preferred_element_type=jnp.float32,
    )
    result = result.reshape(2, z_cells, y_cells, x_cells)
    return (result[0], result[1], log_power)


def solution(mesh):
    torus = Mesh(mesh.devices.reshape(12, 8, 4, 2), ("row_0", "row_1", "col_0", "col_1"))
    in_specs = (P(ROW, COL, None), P())
    out_specs = (P(ROW, COL, None), P(ROW, COL, None), P(COL))
    return jax.shard_map(
        shards, mesh=torus, in_specs=in_specs, out_specs=out_specs, check_vma=False
    )
```

profile of v0, /device:TPU:1, one launch (start us, length us, event | category | flops | bytes accessed | tf_op | source)
XLA Modules:
  0.0 154.7 jit_solution(17920151333053601554)
XLA Ops:
  0.9 7.2 %fusion.5 = (f32[768,1,8,49]{0,3,2,1:T(8,128)}, f32[768,1,8,49]{0,3,2,1:T(8,128)}, f32[768,1,8,49]{0,3,2,1:T(8,128)S(1)}, f32[768,1,8,49]{0,3,2,1:T(8,128)S(1)}) fusion(f32[8,49]{1,0:T(8,128)S(1)} %select_multiply_fusion, s32[8,49]{1,0:T(8,128)S(1)} %iota_add_fusion, f32[8,49]{1,0:T(8,128)S(1)} %fusion.139), kind=kLoop, calls=%fused_computation.10 | loop fusion | flops 4214784 | bytes 4821600 | tf_op jit(solution)/shard_map/mul | solution.py:126
  8.3 1.7 %reshape.630 = f32[768,784]{0,1:T(8,128)} reshape(f32[768,2,8,49]{0,3,2,1:T(8,128)S(1)} %pad_maximum_fusion) | data formatting | bytes 4816896 | tf_op jit(solution)/shard_map/reshape | solution.py:69
  10.0 1.8 %reshape.646 = f32[2,8,49,768,1]{3,2,1,0,4:T(8,128)S(1)} reshape(f32[784,768]{1,0:T(8,128)} %bitcast.194) | data formatting | bytes 4816896 | tf_op jit(solution)/shard_map/dot_general | solution.py:72
  11.9 4.2 %convolution_bitcast_fusion = f32[2,1,12,2,8,49]{5,2,4,3,0,1:T(8,128)S(1)} fusion(f32[2,8,49,768,1]{3,2,1,0,4:T(8,128)S(1)} %reshape.646, f32[1,1,12,768]{3,2,0,1:T(8,128)S(1)} %fusion.29, f32[1,1,12,768]{3,2,0,1:T(8,128)S(1)} %copy.35), kind=kOutput, calls=%fused_computation.15 | convolution fusion | flops 173426688 | bytes 2557440 | tf_op jit(solution)/shard_map/dot_general | solution.py:72
  16.2 1.0 reshape.650
  17.2 13.7 %all-to-all-start = ((f32[8,1,2352]{2,1,0:T(1,128)}), f32[8,1,2352]{2,1,0:T(1,128)S(1)}, u32[]{:S(2)}, u32[]{:S(2)}) async-start(f32[8,1,2352]{2,1,0:T(1,128)} %reshape.650), calls=%async_computation | async-start | bytes 155648 | tf_op jit(solution)/shard_map/all_to_all | solution.py:74
  33.6 2.0 %pad_maximum_fusion.1 = f32[768,2,8,49]{0,3,2,1:T(8,128)S(1)} fusion(f32[768,1,8,49]{0,3,2,1:T(8,128)} %get-tuple-element.21, f32[768,1,8,49]{0,3,2,1:T(8,128)} %get-tuple-element.20), kind=kLoop, calls=%fused_computation.1 | loop fusion | flops 602112 | bytes 4816896 | tf_op jit(solution)/shard_map/stack | solution.py:125
  35.6 1.7 %reshape.642 = f32[768,784]{0,1:T(8,128)} reshape(f32[768,2,8,49]{0,3,2,1:T(8,128)S(1)} %pad_maximum_fusion.1) | data formatting | bytes 4816896 | tf_op jit(solution)/shard_map/reshape | solution.py:127
  41.7 0.9 reshape.652
  42.6 14.0 %all-to-all-start.1 = ((f32[96,1,196]{2,1,0:T(1,128)}), f32[96,1,196]{2,1,0:T(1,128)S(1)}, u32[]{:S(2)}, u32[]{:S(2)}) async-start(f32[96,1,196]{2,1,0:T(1,128)} %reshape.652), calls=%async_computation.1 | async-start | bytes 196608 | tf_op jit(solution)/shard_map/all_to_all | solution.py:80
  56.6 13.7 %all-to-all-done.1 = f32[96,1,196]{2,1,0:T(1,128)S(1)} async-done(((f32[96,1,196]{2,1,0:T(1,128)}), f32[96,1,196]{2,1,0:T(1,128)S(1)}, u32[]{:S(2)}, u32[]{:S(2)}) %all-to-all-start.1) | async-done | bytes 75296 | tf_op jit(solution)/shard_map/all_to_all | solution.py:80
  70.3 0.9 reduce.1
  75.5 0.9 reshape.654
  76.4 5.9 %all-to-all-start.2 = ((f32[96,1,196]{2,1,0:T(1,128)}), f32[96,1,196]{2,1,0:T(1,128)S(1)}, u32[]{:S(2)}, u32[]{:S(2)}) async-start(f32[96,1,196]{2,1,0:T(1,128)} %reshape.654), calls=%async_computation.2 | async-start | bytes 196608 | tf_op jit(solution)/shard_map/all_to_all | solution.py:117
  82.5 19.4 %psum.28 = f32[392]{0:T(512)S(1)} all-reduce(f32[392]{0:T(512)S(1)} %mul.570), channel_id=1, replica_groups=mesh['row_0'=12,'row_1'=8,'col_0'=4,'col_1'=2] {'row_0'}, use_global_device_ids=true, to_apply=%region_1.2 | all-reduce | flops 392 | bytes 3136 | tf_op jit(solution)/shard_map/psum | solution.py:22
  101.9 13.1 %psum.29 = f32[392]{0:T(512)S(1)} all-reduce(f32[392]{0:T(512)S(1)} %psum.28), channel_id=1, replica_groups=mesh['row_0'=12,'row_1'=8,'col_0'=4,'col_1'=2] {'row_1'}, use_global_device_ids=true, to_apply=%region_2.3 | all-reduce | flops 392 | bytes 3136 | tf_op jit(solution)/shard_map/psum | solution.py:22
  115.0 8.2 %psum.30 = f32[392]{0:T(512)S(1)} all-reduce(f32[392]{0:T(512)S(1)} %psum.29), channel_id=1, replica_groups=mesh['row_0'=12,'row_1'=8,'col_0'=4,'col_1'=2] {'col_0'}, use_global_device_ids=true, to_apply=%region_3.4 | all-reduce | flops 392 | bytes 3136 | tf_op jit(solution)/shard_map/psum | solution.py:22
  123.2 14.7 %psum.31 = f32[392]{0:T(512)S(1)} all-reduce(f32[392]{0:T(512)S(1)} %psum.30), channel_id=1, replica_groups=mesh['row_0'=12,'row_1'=8,'col_0'=4,'col_1'=2] {'col_1'}, use_global_device_ids=true, to_apply=%region_4.5 | all-reduce | flops 392 | bytes 3136 | tf_op jit(solution)/shard_map/psum | solution.py:22
  137.9 0.9 reduce.2
  141.0 1.0 reshape.656
  142.0 3.6 %all-to-all-start.3 = ((f32[8,1,2352]{2,1,0:T(1,128)}), f32[8,1,2352]{2,1,0:T(1,128)S(1)}, u32[]{:S(2)}, u32[]{:S(2)}) async-start(f32[8,1,2352]{2,1,0:T(1,128)} %reshape.656), calls=%async_computation.3 | async-start | bytes 155648 | tf_op jit(solution)/shard_map/all_to_all | solution.py:122
  145.6 1.2 compare_select_fusion
  146.9 3.7 %all-to-all-done.3 = f32[8,1,2352]{2,1,0:T(1,128)S(1)} async-done(((f32[8,1,2352]{2,1,0:T(1,128)}), f32[8,1,2352]{2,1,0:T(1,128)S(1)}, u32[]{:S(2)}, u32[]{:S(2)}) %all-to-all-start.3) | async-done | bytes 75296 | tf_op jit(solution)/shard_map/all_to_all | solution.py:122
  152.0 1.4 fusion.202
  (67 shorter events, 15.0 us)
Async XLA Ops:
  10.0 1.8 %copy-start.1 = (f32[1,12,768]{2,0,1:T(1,128)S(1)}, f32[1,12,768]{2,0,1:T(1,128)}, u32[]{:S(2)}) copy-start(f32[1,12,768]{2,0,1:T(1,128)} %param.2) | copy-start | bytes 110596
  11.9 19.1 %copy-start.2 = (s32[8]{0:T(128)S(1)}, s32[8]{0:T(128)}, u32[]{:S(2)}) copy-start(s32[8]{0:T(128)} %param.3) | copy-start | bytes 100
  17.2 20.7 %all-to-all-start = ((f32[8,1,2352]{2,1,0:T(1,128)}), f32[8,1,2352]{2,1,0:T(1,128)S(1)}, u32[]{:S(2)}, u32[]{:S(2)}) async-start(f32[8,1,2352]{2,1,0:T(1,128)} %reshape.650), calls=%async_computation | async-start | bytes 155648 | tf_op jit(solution)/shard_map/all_to_all | solution.py:74
  42.6 27.7 %all-to-all-start.1 = ((f32[96,1,196]{2,1,0:T(1,128)}), f32[96,1,196]{2,1,0:T(1,128)S(1)}, u32[]{:S(2)}, u32[]{:S(2)}) async-start(f32[96,1,196]{2,1,0:T(1,128)} %reshape.652), calls=%async_computation.1 | async-start | bytes 196608 | tf_op jit(solution)/shard_map/all_to_all | solution.py:80
  76.4 61.5 %all-to-all-start.2 = ((f32[96,1,196]{2,1,0:T(1,128)}), f32[96,1,196]{2,1,0:T(1,128)S(1)}, u32[]{:S(2)}, u32[]{:S(2)}) async-start(f32[96,1,196]{2,1,0:T(1,128)} %reshape.654), calls=%async_computation.2 | async-start | bytes 196608 | tf_op jit(solution)/shard_map/all_to_all | solution.py:117
  140.0 12.0 %copy-start = (f32[768,784]{0,1:T(8,128)S(1)}, f32[768,784]{0,1:T(8,128)}, u32[]{:S(2)}) copy-start(f32[768,784]{0,1:T(8,128)} %reshape.642) | copy-start | bytes 7225348
  142.0 8.5 %all-to-all-start.3 = ((f32[8,1,2352]{2,1,0:T(1,128)}), f32[8,1,2352]{2,1,0:T(1,128)S(1)}, u32[]{:S(2)}, u32[]{:S(2)}) async-start(f32[8,1,2352]{2,1,0:T(1,128)} %reshape.656), calls=%async_computation.3 | async-start | bytes 155648 | tf_op jit(solution)/shard_map/all_to_all | solution.py:122
where the time goes:
time: 155 us
  blocking collectives  55.4 us (36%)
  starting transfers between devices  37.2 us (24%)
  waiting for transfers between devices  17.4 us (11%)
  other arithmetic  14.9 us (10%)
  local copies, waits for them, and re-layouts  14.4 us (9%)
  matrix products  12.3 us (8%)
  between operations  3.03 us (2%)
    psum x4, blocking collectives, one_axis_at_a_time(): shard = lax.psum(shard, axis)  55.4 us
    all_to_all x1, starting transfers between devices, shards(): lax.all_to_all(spectra, ROW, split_axis=2, concat_axis=1, tiled=True)  14 us
    all_to_all x1, starting transfers between devices, shards(): lax.all_to_all(spectra, COL, split_axis=4, concat_axis=2, tiled=True)  13.7 us
    all_to_all x1, waiting for transfers between devices, shards(): lax.all_to_all(spectra, ROW, split_axis=2, concat_axis=1, tiled=True)  13.7 us
    mul x1, other arithmetic, shards(): jnp.cos(phases) * weights  7.24 us
    unnamed x16, local copies, waits for them, and re-layouts  6.14 us
    all_to_all x1, starting transfers between devices, shards(): lax.all_to_all(new_fields, ROW, split_axis=1, concat_axis=2, tiled=True)  5.91 us
    dot_general x1, matrix products, shards(): jnp.dot(fields, forward_table, precision=highest, preferred_element_type=...  4.19 us
  transfers between devices with their start and end apart: 4, of which 2 were waited for; matrix products, arithmetic and copies ran while one was open for 4% of the time, Pallas kernels for 0%

commit v1 on v0

v1 whole, which is shorter than its diff:
```python
import functools
import math

import jax
import jax.numpy as jnp
import numpy as np
from jax import lax
from jax.experimental import pallas as pl
from jax.experimental.pallas import tpu as pltpu
from jax.sharding import PartitionSpec as P

MESH = pl.DeviceIdType.MESH
NX, NY, NZ = 768, 96, 96
HALF = NX // 2
COLS, ROWS = 8, 96
YB = NY // COLS
LANES = 128
SLOTS = 64
EVEN, ODD = 49, 48
SPARE = 15
PLANES = NX // 2 + 1
KX_MOST = 73
BLOCK = 2 * YB
WIDE = 2 * NY

time_step = 16.0
grad_coeff = 1.0
power_floor = 1e-6


def split(table):
    high = table.astype(np.float32).astype(jnp.bfloat16)
    low = (table - high.astype(np.float64)).astype(np.float32).astype(jnp.bfloat16)
    return np.stack([high, low])


def plane_of(col, slot):
    even = 2 * (EVEN * col + slot)
    odd = 2 * (ODD * (col - COLS // 2) + slot) + 1
    in_even = (slot < EVEN) & (even < PLANES)
    in_odd = slot < ODD
    low_col = col < COLS // 2
    return np.where(low_col, np.where(in_even, even, -1), np.where(in_odd, odd, -1))


@functools.cache
def tables():
    col = np.arange(COLS)[:, None]
    slot = np.arange(SLOTS)[None, :]
    plane = plane_of(col, slot)
    used = plane >= 0
    cells = np.arange(HALF)[:, None, None]
    phase = 2.0 * math.pi / NX * ((cells * np.maximum(plane, 0)[None]) % NX)
    x_table = np.stack([np.cos(phase) * used, -np.sin(phase) * used], axis=2)
    x_table = x_table.reshape(HALF, 2, COLS // 2 * LANES).transpose(1, 0, 2)
    edge = (plane == 0) | (2 * plane == NX)
    weight = np.where(used, np.where(edge, 1.0, 2.0), 0.0) / float(NX * NY * NZ)
    weight = np.concatenate([weight, weight], axis=1).reshape(COLS, 1, LANES)

    index = np.arange(96)
    phase = 2.0 * math.pi / 96 * ((index[:, None] * index[None, :]) % 96)
    cosine, sine = np.cos(phase), np.sin(phase)
    full = np.stack([np.stack([cosine, sine], 1), np.stack([-sine, cosine], 1)])
    full = full.reshape(2, 96, 2, 96)
    by_block = full.reshape(2, 96, 2, COLS, YB)
    y_forward = by_block.transpose(1, 0, 3, 2, 4).reshape(WIDE, WIDE)
    z_forward = full.transpose(0, 1, 3, 2).reshape(WIDE, WIDE)
    square = np.stack([split(y_forward), split(z_forward), split(z_forward.T), split(y_forward.T)])

    lane = np.arange(LANES)[None, None, :]
    part = np.arange(2)[None, :, None]
    inside = lane % SLOTS
    packed = SPARE * (2 * part + lane // SLOTS) + inside - EVEN
    ids = plane_of(np.arange(COLS)[:, None, None], packed)
    ids = np.where((inside >= EVEN) & (packed < EVEN), ids, -1).astype(np.int32).reshape(2 * COLS, LANES)
    return (
        np.stack([split(x_table[0]), split(x_table[1])]),
        square,
        weight.astype(np.float32),
        ids,
    )


def halves(value):
    high = value.astype(jnp.bfloat16)
    low = (value - high.astype(jnp.float32)).astype(jnp.bfloat16)
    return high, low


def product(a, b, contract):
    return lax.dot_general(a, b, (contract, ((), ())), preferred_element_type=jnp.float32)


def table_times(table, value):
    high, low = halves(value)
    inner = ((1,), (0,))
    return product(table[0], high, inner) + (product(table[1], high, inner) + product(table[0], low, inner))


def times_table(value, table, contract):
    high, low = halves(value)
    return product(high, table[0], contract) + (product(low, table[0], contract) + product(high, table[1], contract))


def signal(semaphore, row, col):
    pl.semaphore_signal(semaphore, inc=1, device_id=(row, col), device_id_type=MESH)


def col_exchange(source, target, send, receive, row, col):
    mine = pl.ds(pl.multiple_of(col * BLOCK, 8), BLOCK)
    for step in range(1, COLS):
        peer = lax.rem(col + step, COLS)
        theirs = pl.ds(pl.multiple_of(peer * BLOCK, 8), BLOCK)
        pltpu.make_async_remote_copy(
            source.at[theirs], target.at[mine], send, receive, device_id=(row, peer), device_id_type=MESH
        ).start()
    pltpu.make_async_copy(source.at[mine], target.at[mine], receive).start()


def row_exchange(source, target, send, receive, row, col):
    mine = pl.ds(2 * row, 2)

    def one(step, carry):
        peer = lax.rem(row + step, ROWS)
        pltpu.make_async_remote_copy(
            source.at[pl.ds(2 * peer, 2)], target.at[mine], send, receive, device_id=(peer, col), device_id_type=MESH
        ).start()
        return carry

    lax.fori_loop(1, ROWS, one, 0)
    pltpu.make_async_copy(source.at[mine], target.at[mine], receive).start()


def arrived(buffer, semaphore):
    pltpu.make_async_copy(buffer, buffer, semaphore).wait()


def kernel(
    counts, cells, x_hbm, square_hbm, weight, ids, conc_out, chem_out, power_out,
    x_table, square, buffers, table_sems, send_sems, recv_sems,
):
    row, col = lax.axis_index("row"), lax.axis_index("col")
    barrier = pltpu.get_barrier_semaphore()

    def greet(step, carry):
        signal(barrier, lax.rem(row + step, ROWS), col)
        return carry

    for step in range(1, COLS):
        signal(barrier, row, lax.rem(col + step, COLS))
    lax.fori_loop(1, ROWS, greet, 0)
    loads = [
        pltpu.make_async_copy(x_hbm.at[0], x_table.at[0], table_sems.at[0]),
        pltpu.make_async_copy(x_hbm.at[1], x_table.at[1], table_sems.at[1]),
        pltpu.make_async_copy(square_hbm, square, table_sems.at[2]),
    ]
    for load in loads:
        load.start()

    lane = lax.broadcasted_iota(jnp.int32, (16, LANES), 1)
    first = lane < SLOTS
    conc = jnp.concatenate([cells[:, 0, :], jnp.zeros((16 - YB, NX), jnp.float32)])
    chem = conc * conc * conc - conc
    both = jnp.concatenate([conc, chem])
    folded = (both[:, :HALF] + both[:, HALF:], both[:, :HALF] - both[:, HALF:])
    out = buffers.at[0]
    for parity in range(2):
        loads[parity].wait()
        spectrum = times_table(folded[parity], x_table.at[parity], ((1,), (0,)))
        for j in range(COLS // 2):
            part = spectrum[:, j * LANES:(j + 1) * LANES]
            top, bottom = part[:16], part[16:]
            base = (parity * (COLS // 2) + j) * BLOCK
            real = jnp.where(first, top, pltpu.roll(bottom, SLOTS, 1))
            imag = jnp.where(first, pltpu.roll(top, SLOTS, 1), bottom)
            out[base:base + YB, :] = real[:YB]
            out[base + YB:base + BLOCK, :] = imag[:YB]

    pl.semaphore_wait(barrier, COLS - 1 + ROWS - 1)
    col_exchange(buffers.at[0], buffers.at[1], send_sems.at[0], recv_sems.at[0], row, col)
    loads[2].wait()

    lane_w = lax.broadcasted_iota(jnp.int32, (NZ, LANES), 1)
    kz = lax.broadcasted_iota(jnp.int32, (NZ, LANES), 0)
    slot = lax.rem(lane_w, SLOTS)
    low_col = col < COLS // 2
    kx = 2 * slot + jnp.where(low_col, 2 * EVEN * col, 2 * ODD * (col - COLS // 2) + 1)
    x_wave = kx.astype(jnp.float32) * (2.0 * math.pi / NX)
    y_wave = jnp.minimum(row, NY - row).astype(jnp.float32) * (2.0 * math.pi / NY)
    z_wave = jnp.minimum(kz, NZ - kz).astype(jnp.float32) * (2.0 * math.pi / NZ)
    squared = z_wave * z_wave + y_wave * y_wave + x_wave * x_wave
    damping = 1.0 / (1.0 + time_step * grad_coeff * squared * squared)
    mixing = jnp.where(lane_w < SLOTS, -time_step * squared, grad_coeff * squared)

    arrived(buffers.at[1], recv_sems.at[0])
    buffers[2] = table_times(square.at[0], buffers[1])
    row_exchange(buffers.at[2], buffers.at[3], send_sems.at[1], recv_sems.at[1], row, col)
    arrived(buffers.at[3], recv_sems.at[1])
    hat = table_times(square.at[1], buffers[3])
    real, imag = hat[:NZ], hat[NZ:]
    real = (real + mixing * pltpu.roll(real, SLOTS, 1)) * damping
    imag = (imag + mixing * pltpu.roll(imag, SLOTS, 1)) * damping
    partial = jnp.sum(real * real + imag * imag, axis=0, keepdims=True)
    partial = jnp.broadcast_to(partial, (8, LANES))
    lane_8 = lax.broadcasted_iota(jnp.int32, (8, LANES), 1)
    sub_8 = lax.broadcasted_iota(jnp.int32, (8, LANES), 0)
    spare_8 = lax.rem(lane_8, SLOTS) >= EVEN
    chunks = [
        pltpu.roll(partial, (EVEN + SLOTS * (k % 2) - SPARE * k) % LANES, 1) for k in range(4)
    ]
    packed = jnp.where(
        lax.rem(sub_8, 2) == 0,
        jnp.where(lane_8 < SLOTS, chunks[0], chunks[1]),
        jnp.where(lane_8 < SLOTS, chunks[2], chunks[3]),
    )
    field = table_times(square.at[2], jnp.concatenate([real, imag])).reshape(WIDE // 8, 8, LANES)
    buffers[4] = jnp.where(spare_8[None], packed[None], field).reshape(WIDE, LANES)
    row_exchange(buffers.at[4], buffers.at[5], send_sems.at[2], recv_sems.at[2], row, col)
    arrived(buffers.at[5], recv_sems.at[2])
    gathered = buffers[5]
    total = jnp.sum(gathered.reshape(WIDE // 8, 8, LANES), axis=0)
    total = total + pltpu.roll(total, 2, 0)
    total = total + pltpu.roll(total, 4, 0)
    even_total = jnp.broadcast_to(total[0:1], (BLOCK, LANES))
    odd_total = jnp.broadcast_to(total[1:2], (BLOCK, LANES))
    sub_b = lax.broadcasted_iota(jnp.int32, (BLOCK, LANES), 0)
    lane_b = lax.broadcasted_iota(jnp.int32, (BLOCK, LANES), 1)
    totals = jnp.where(sub_b < YB, even_total, odd_total)
    spare_b = lax.rem(lane_b, SLOTS) >= EVEN
    field = table_times(square.at[3], gathered).reshape(COLS, BLOCK, LANES)
    buffers[6] = jnp.where(spare_b[None], totals[None], field).reshape(WIDE, LANES)
    col_exchange(buffers.at[6], buffers.at[7], send_sems.at[3], recv_sems.at[3], row, col)

    start = jnp.int32(0)
    for i in range(COLS):
        start = start + jnp.where(i < col, counts[i], 0)
    mine = counts[col]
    wanted = lax.broadcasted_iota(jnp.int32, (80, LANES), 0) + start

    arrived(buffers.at[7], recv_sems.at[3])
    last = buffers.at[7]
    sums = []
    for parity in range(2):
        pieces = []
        for j in range(COLS // 2):
            c = parity * (COLS // 2) + j
            pad = jnp.zeros((16 - YB, LANES), jnp.float32)
            real = jnp.concatenate([last[c * BLOCK:c * BLOCK + YB, :], pad])
            imag = jnp.concatenate([last[c * BLOCK + YB:(c + 1) * BLOCK, :], pad])
            scale = weight[c]
            keep = scale > 0.0
            top = jnp.where(first, real, pltpu.roll(imag, SLOTS, 1))
            bottom = jnp.where(first, pltpu.roll(real, SLOTS, 1), imag)
            pieces.append(jnp.where(keep, jnp.concatenate([top, bottom]) * scale, 0.0))
        sums.append(times_table(jnp.concatenate(pieces, axis=1), x_table.at[parity], ((1,), (1,))))
    front, back = sums[0] + sums[1], sums[0] - sums[1]
    conc_out[:, 0, :HALF] = front[:YB]
    conc_out[:, 0, HALF:] = back[:YB]
    chem_out[:, 0, :HALF] = front[16:16 + YB]
    chem_out[:, 0, HALF:] = back[16:16 + YB]

    found = jnp.zeros((80, LANES), jnp.float32)
    for c in range(COLS):
        for part in range(2):
            at = c * BLOCK + part * YB
            values = jnp.broadcast_to(last[at:at + 1, :], (80, LANES))
            found = found + jnp.where(ids[2 * c + part:2 * c + part + 1, :] == wanted, values, 0.0)
    power = lax.dot_general(
        jnp.ones((8, LANES), jnp.float32), found, (((1,), (1,)), ((), ())),
        precision=lax.Precision.HIGHEST, preferred_element_type=jnp.float32,
    )
    power = jnp.log(power * (1.0 / float(NX * NY * NY * NZ * NZ)) + power_floor)
    power = jnp.where(lax.broadcasted_iota(jnp.int32, (8, 80), 1) < mine, power, 0.0)
    power_out[...] = power[0:1, :KX_MOST]

    for i, (buffer, left) in enumerate(((0, BLOCK), (2, 2), (4, 2), (6, BLOCK))):
        sent = buffers.at[buffer, pl.ds(0, WIDE - left)]
        arrived(sent, send_sems.at[i])


def shards(concentration, plane_counts):
    x_table, square, weight, ids = (jnp.asarray(t) for t in tables())
    vmem = pl.BlockSpec(memory_space=pltpu.VMEM)
    anywhere = pl.BlockSpec(memory_space=pl.ANY)
    smem = pl.BlockSpec(memory_space=pltpu.SMEM)
    conc, chem, power = pl.pallas_call(
        kernel,
        out_shape=(
            jax.ShapeDtypeStruct((YB, 1, NX), jnp.float32),
            jax.ShapeDtypeStruct((YB, 1, NX), jnp.float32),
            jax.ShapeDtypeStruct((1, KX_MOST), jnp.float32),
        ),
        in_specs=[smem, vmem, anywhere, anywhere, vmem, vmem],
        out_specs=(vmem, vmem, vmem),
        scratch_shapes=[
            pltpu.VMEM(x_table.shape, jnp.bfloat16),
            pltpu.VMEM(square.shape, jnp.bfloat16),
            pltpu.VMEM((8, WIDE, LANES), jnp.float32),
            pltpu.SemaphoreType.DMA((3,)),
            pltpu.SemaphoreType.DMA((4,)),
            pltpu.SemaphoreType.DMA((4,)),
        ],
        compiler_params=pltpu.CompilerParams(collective_id=0, has_side_effects=True),
    )(plane_counts, concentration.reshape(YB, 1, NX), x_table, square, weight, ids)
    return conc.reshape(1, YB, NX), chem.reshape(1, YB, NX), power.reshape(KX_MOST)


def solution(mesh):
    return jax.shard_map(
        shards,
        mesh=mesh,
        in_specs=(P("row", "col", None), P()),
        out_specs=(P("row", "col", None), P("row", "col", None), P("col")),
        check_vma=False,
    )
```

time: 155 us -> 58.2 us (0.38)
  blocking collectives: 55.4 us -> 0 us
  Pallas kernels: 0 us -> 53.3 us
  starting transfers between devices: 37.2 us -> 0 us
  waiting for transfers between devices: 17.4 us -> 0 us
  other arithmetic: 14.9 us -> 0 us
  matrix products: 12.3 us -> 0 us
  local copies, waits for them, and re-layouts: 14.4 us -> 3.98 us
  between operations: 3.03 us -> 0.64 us
    psum x4 -> x0, blocking collectives: 55.4 us -> none  [one_axis_at_a_time(): shard = lax.psum(shard, axis)]
    pallas_call x0 -> x1, Pallas kernels: none -> 53.3 us  [shards(): pl.pallas_call(kernel, out_shape=(jax.ShapeDtypeStruct((YB, 1, NX), jnp.f...]
    all_to_all x4 -> x0, starting transfers between devices: 37.2 us -> none  [the longest x1 14 us: shards(): lax.all_to_all(spectra, ROW, split_axis=2, concat_axis=1, tiled=True)]
    all_to_all x4 -> x0, waiting for transfers between devices: 17.4 us -> none  [the longest x1 13.7 us: shards(): lax.all_to_all(spectra, ROW, split_axis=2, concat_axis=1, tiled=True)]
    dot_general x18 -> x0, matrix products: 12.3 us -> none  [the longest x1 4.19 us: shards(): jnp.dot(fields, forward_table, precision=highest, preferred_element_type=...]
    mul x2 -> x0, other arithmetic: 7.31 us -> none  [the longest x1 7.24 us: shards(): jnp.cos(phases) * weights]
    reshape x4 -> x0, local copies, waits for them, and re-layouts: 3.62 us -> none  [the longest x1 1.67 us: shards(): forward_table = jnp.stack([jnp.cos(phases) * in_use, -jnp.sin(phases) * i...]
    all_to_all x4 -> x0, other arithmetic: 3.41 us -> none  [the longest x1 0.88 us: shards(): lax.all_to_all(new_fields, ROW, split_axis=1, concat_axis=2, tiled=True)]
  transfers between devices with their start and end apart: 4 -> 0, of which waited for: 2 -> 0; matrix products, arithmetic and copies ran while one was open for 4% -> 0% of each run, Pallas kernels for 0% -> 0%
where the time goes in v1:
time: 58.2 us; the launch traced here: 57.9 us
  Pallas kernels  53.3 us (92%)
  local copies, waits for them, and re-layouts  3.98 us (7%)
  between operations  0.64 us (1%)
    pallas_call x1, Pallas kernels, shards(): pl.pallas_call(kernel, out_shape=(jax.ShapeDtypeStruct((YB, 1, NX), jnp.f...  53.3 us
    unnamed x3, local copies, waits for them, and re-layouts  3.98 us

profile of v1, /device:TPU:1, one launch (start us, length us, event | category | flops | bytes accessed | tf_op | source)
XLA Modules:
  0.0 57.9 jit_solution(5460268583681774482)
XLA Ops:
  0.6 53.3 %shard_map.85 = (f32[12,1,768]{2,1,0:T(1,128)}, f32[12,1,768]{2,1,0:T(1,128)}, f32[1,73]{1,0:T(1,128)}) custom-call(s32[8]{0:T(128)} %counts.1, f32[12,1,768]{2,1,0:T(1,128)} %bitcast.6, bf16[2,2,384,512]{3,2,1,0:T(8,128)(2,1)} %constant.8.clone.x_hbm, bf16[4,2,192,192]{3,2,1,0:T(8,128)(2,1)} %constant.9.clone.square_hbm, ...), custom_call_target="tpu_custom_call" | custom-call | tf_op jit(solution)/shard_map/pallas_call | solution.py:286
  53.9 1.4 %copy.12 = f32[1,12,768]{2,0,1:T(1,128)} copy(f32[1,12,768]{2,0,1:T(1,128)} %bitcast.5) | data formatting | bytes 73728
  55.3 1.4 %copy.13 = f32[1,12,768]{2,0,1:T(1,128)} copy(f32[1,12,768]{2,0,1:T(1,128)} %bitcast.4) | data formatting | bytes 73728
  56.7 1.2 %copy.14 = f32[73]{0:T(128)} copy(f32[73]{0:T(128)} %bitcast.7) | data formatting | bytes 584

commit v2 on v1

--- a/solution.py
+++ b/solution.py
@@ -13,6 +13,10 @@
 NX, NY, NZ = 768, 96, 96
 HALF = NX // 2
 COLS, ROWS = 8, 96
+RING_Z, RING_Y = 12, 8
+FAR_Y = (4, 3, 5, 2, 6, 1, 7)
+NEAR_Z = (1, 2, 3, -1, -2, -3)
+NEAR_Y = (1, 2, -1, -2)
 YB = NY // COLS
 LANES = 128
 SLOTS = 64
@@ -22,6 +26,9 @@
 KX_MOST = 73
 BLOCK = 2 * YB
 WIDE = 2 * NY
+X_SHARE = COLS // 2 * LANES
+VMEM = 67_043_328
+ROOM = 10_600_000
 
 time_step = 16.0
 grad_coeff = 1.0
@@ -34,7 +41,7 @@
     return np.stack([high, low])
 
 
-def plane_of(col, slot):
+def plane_of(col, slot, np=np):
     even = 2 * (EVEN * col + slot)
     odd = 2 * (ODD * (col - COLS // 2) + slot) + 1
     in_even = (slot < EVEN) & (even < PLANES)
@@ -53,9 +60,6 @@
     phase = 2.0 * math.pi / NX * ((cells * np.maximum(plane, 0)[None]) % NX)
     x_table = np.stack([np.cos(phase) * used, -np.sin(phase) * used], axis=2)
     x_table = x_table.reshape(HALF, 2, COLS // 2 * LANES).transpose(1, 0, 2)
-    edge = (plane == 0) | (2 * plane == NX)
-    weight = np.where(used, np.where(edge, 1.0, 2.0), 0.0) / float(NX * NY * NZ)
-    weight = np.concatenate([weight, weight], axis=1).reshape(COLS, 1, LANES)
 
     index = np.arange(96)
     phase = 2.0 * math.pi / 96 * ((index[:, None] * index[None, :]) % 96)
@@ -65,20 +69,10 @@
     by_block = full.reshape(2, 96, 2, COLS, YB)
     y_forward = by_block.transpose(1, 0, 3, 2, 4).reshape(WIDE, WIDE)
     z_forward = full.transpose(0, 1, 3, 2).reshape(WIDE, WIDE)
-    square = np.stack([split(y_forward), split(z_forward), split(z_forward.T), split(y_forward.T)])
-
-    lane = np.arange(LANES)[None, None, :]
-    part = np.arange(2)[None, :, None]
-    inside = lane % SLOTS
-    packed = SPARE * (2 * part + lane // SLOTS) + inside - EVEN
-    ids = plane_of(np.arange(COLS)[:, None, None], packed)
-    ids = np.where((inside >= EVEN) & (packed < EVEN), ids, -1).astype(np.int32).reshape(2 * COLS, LANES)
-    return (
-        np.stack([split(x_table[0]), split(x_table[1])]),
-        square,
-        weight.astype(np.float32),
-        ids,
-    )
+    square = np.zeros((2, HALF, X_SHARE), jnp.bfloat16)
+    for k, table in enumerate((y_forward, z_forward, z_forward.T, y_forward.T)):
+        square[:, k // 2 * WIDE:(k // 2 + 1) * WIDE, k % 2 * 256:k % 2 * 256 + WIDE] = split(table)
+    return np.concatenate([split(x_table[0]), split(x_table[1]), square])
 
 
 def halves(value):
@@ -119,15 +113,23 @@
 
 def row_exchange(source, target, send, receive, row, col):
     mine = pl.ds(2 * row, 2)
-
-    def one(step, carry):
-        peer = lax.rem(row + step, ROWS)
+    row_z, row_y = row // RING_Y, lax.rem(row, RING_Y)
+
+    def one(step_z, step_y):
+        peer = lax.rem(row_z + step_z, RING_Z) * RING_Y + lax.rem(row_y + step_y, RING_Y)
         pltpu.make_async_remote_copy(
             source.at[pl.ds(2 * peer, 2)], target.at[mine], send, receive, device_id=(peer, col), device_id_type=MESH
         ).start()
+
+    def plane(i, carry):
+        step_z = RING_Z // 2 + (1 - 2 * lax.rem(i, 2)) * ((i + 1) // 2)
+        for step_y in FAR_Y + (0,):
+            one(step_z, step_y)
         return carry
 
-    lax.fori_loop(1, ROWS, one, 0)
+    lax.fori_loop(0, RING_Z - 1, plane, 0)
+    for step_y in FAR_Y:
+        one(0, step_y)
     pltpu.make_async_copy(source.at[mine], target.at[mine], receive).start()
 
 
@@ -135,37 +137,40 @@
     pltpu.make_async_copy(buffer, buffer, semaphore).wait()
 
 
-def kernel(
-    counts, cells, x_hbm, square_hbm, weight, ids, conc_out, chem_out, power_out,
-    x_table, square, buffers, table_sems, send_sems, recv_sems,
+def spectral(
+    cells_hbm, tables_hbm, conc_out, chem_out, total_out,
+    cells, x_table, square, buffers, load_sems, send_sems, recv_sems, near_z, near_y, ring_y,
 ):
     row, col = lax.axis_index("row"), lax.axis_index("col")
+    row_z, row_y = row // RING_Y, lax.rem(row, RING_Y)
+    loads = [
+        pltpu.make_async_copy(cells_hbm, cells, load_sems.at[0]),
+        pltpu.make_async_copy(tables_hbm.at[pl.ds(0, 2)], x_table.at[0], load_sems.at[1]),
+        pltpu.make_async_copy(tables_hbm.at[pl.ds(2, 2)], x_table.at[1], load_sems.at[2]),
+        pltpu.make_async_copy(tables_hbm.at[pl.ds(4, 2)], square, load_sems.at[3]),
+    ]
     barrier = pltpu.get_barrier_semaphore()
-
-    def greet(step, carry):
-        signal(barrier, lax.rem(row + step, ROWS), col)
-        return carry
-
+    at_z = [lax.rem(row_z + RING_Z + step, RING_Z) * RING_Y + row_y for step in NEAR_Z]
+    at_y = [row_z * RING_Y + lax.rem(row_y + RING_Y + step, RING_Y) for step in NEAR_Y]
+    around = [row_z * RING_Y + lax.rem(row_y + step, RING_Y) for step in FAR_Y]
+    loads[0].start()
+    for peer in at_z + at_y:
+        signal(barrier, peer, col)
     for step in range(1, COLS):
         signal(barrier, row, lax.rem(col + step, COLS))
-    lax.fori_loop(1, ROWS, greet, 0)
-    loads = [
-        pltpu.make_async_copy(x_hbm.at[0], x_table.at[0], table_sems.at[0]),
-        pltpu.make_async_copy(x_hbm.at[1], x_table.at[1], table_sems.at[1]),
-        pltpu.make_async_copy(square_hbm, square, table_sems.at[2]),
-    ]
-    for load in loads:
+    for load in loads[1:]:
         load.start()
 
     lane = lax.broadcasted_iota(jnp.int32, (16, LANES), 1)
     first = lane < SLOTS
+    loads[0].wait()
     conc = jnp.concatenate([cells[:, 0, :], jnp.zeros((16 - YB, NX), jnp.float32)])
     chem = conc * conc * conc - conc
     both = jnp.concatenate([conc, chem])
     folded = (both[:, :HALF] + both[:, HALF:], both[:, :HALF] - both[:, HALF:])
     out = buffers.at[0]
     for parity in range(2):
-        loads[parity].wait()
+        loads[1 + parity].wait()
         spectrum = times_table(folded[parity], x_table.at[parity], ((1,), (0,)))
         for j in range(COLS // 2):
             part = spectrum[:, j * LANES:(j + 1) * LANES]
@@ -176,9 +181,18 @@
             out[base:base + YB, :] = real[:YB]
             out[base + YB:base + BLOCK, :] = imag[:YB]
 
-    pl.semaphore_wait(barrier, COLS - 1 + ROWS - 1)
+    pl.semaphore_wait(barrier, len(at_z) + len(at_y) + COLS - 1)
     col_exchange(buffers.at[0], buffers.at[1], send_sems.at[0], recv_sems.at[0], row, col)
-    loads[2].wait()
+    for peer in at_z:
+        signal(near_z, peer, col)
+    for peer in at_y:
+        signal(near_y, peer, col)
+    loads[3].wait()
+
+
+    def middle(k):
+        rows, lanes = pl.ds(k // 2 * WIDE, WIDE), pl.ds(k % 2 * 256, WIDE)
+        return square[0, rows, lanes], square[1, rows, lanes]
 
     lane_w = lax.broadcasted_iota(jnp.int32, (NZ, LANES), 1)
     kz = lax.broadcasted_iota(jnp.int32, (NZ, LANES), 0)
@@ -192,11 +206,16 @@
     damping = 1.0 / (1.0 + time_step * grad_coeff * squared * squared)
     mixing = jnp.where(lane_w < SLOTS, -time_step * squared, grad_coeff * squared)
 
+    pl.semaphore_wait(near_z, len(at_z))
+    pl.semaphore_wait(near_y, len(at_y))
+    for peer in around:
+        signal(ring_y, peer, col)
     arrived(buffers.at[1], recv_sems.at[0])
-    buffers[2] = table_times(square.at[0], buffers[1])
+    buffers[2] = table_times(middle(0), buffers[1])
+    pl.semaphore_wait(ring_y, len(around))
     row_exchange(buffers.at[2], buffers.at[3], send_sems.at[1], recv_sems.at[1], row, col)
     arrived(buffers.at[3], recv_sems.at[1])
-    hat = table_times(square.at[1], buffers[3])
+    hat = table_times(middle(1), buffers[3])
     real, imag = hat[:NZ], hat[NZ:]
     real = (real + mixing * pltpu.roll(real, SLOTS, 1)) * damping
     imag = (imag + mixing * pltpu.roll(imag, SLOTS, 1)) * damping
@@ -213,7 +232,7 @@
         jnp.where(lane_8 < SLOTS, chunks[0], chunks[1]),
         jnp.where(lane_8 < SLOTS, chunks[2], chunks[3]),
     )
-    field = table_times(square.at[2], jnp.concatenate([real, imag])).reshape(WIDE // 8, 8, LANES)
+    field = table_times(middle(2), jnp.concatenate([real, imag])).reshape(WIDE // 8, 8, LANES)
     buffers[4] = jnp.where(spare_8[None], packed[None], field).reshape(WIDE, LANES)
     row_exchange(buffers.at[4], buffers.at[5], send_sems.at[2], recv_sems.at[2], row, col)
     arrived(buffers.at[5], recv_sems.at[2])
@@ -227,18 +246,14 @@
     lane_b = lax.broadcasted_iota(jnp.int32, (BLOCK, LANES), 1)
     totals = jnp.where(sub_b < YB, even_total, odd_total)
     spare_b = lax.rem(lane_b, SLOTS) >= EVEN
-    field = table_times(square.at[3], gathered).reshape(COLS, BLOCK, LANES)
+    field = table_times(middle(3), gathered).reshape(COLS, BLOCK, LANES)
     buffers[6] = jnp.where(spare_b[None], totals[None], field).reshape(WIDE, LANES)
     col_exchange(buffers.at[6], buffers.at[7], send_sems.at[3], recv_sems.at[3], row, col)
 
-    start = jnp.int32(0)
-    for i in range(COLS):
-        start = start + jnp.where(i < col, counts[i], 0)
-    mine = counts[col]
-    wanted = lax.broadcasted_iota(jnp.int32, (80, LANES), 0) + start
-
-    arrived(buffers.at[7], recv_sems.at[3])
+    lane_1 = lax.broadcasted_iota(jnp.int32, (1, LANES), 1)
+    slot_1 = lax.rem(lane_1, SLOTS)
     last = buffers.at[7]
+    arrived(last, recv_sems.at[3])
     sums = []
     for parity in range(2):
         pieces = []
@@ -247,8 +262,10 @@
             pad = jnp.zeros((16 - YB, LANES), jnp.float32)
             real = jnp.concatenate([last[c * BLOCK:c * BLOCK + YB, :], pad])
             imag = jnp.concatenate([last[c * BLOCK + YB:(c + 1) * BLOCK, :], pad])
-            scale = weight[c]
-            keep = scale > 0.0
+            plane = plane_of(c, slot_1, jnp)
+            keep = plane >= 0
+            edge = (plane == 0) | (plane == NX // 2)
+            scale = jnp.where(edge, 1.0, 2.0) / float(NX * NY * NZ)
             top = jnp.where(first, real, pltpu.roll(imag, SLOTS, 1))
             bottom = jnp.where(first, pltpu.roll(real, SLOTS, 1), imag)
             pieces.append(jnp.where(keep, jnp.concatenate([top, bottom]) * scale, 0.0))
@@ -259,49 +276,85 @@
     chem_out[:, 0, :HALF] = front[16:16 + YB]
     chem_out[:, 0, HALF:] = back[16:16 + YB]
 
+    for c in range(COLS):
+        for part in range(2):
+            at = c * BLOCK + part * YB
+            total_out[2 * c + part:2 * c + part + 1, :] = last[at:at + 1, :]
+
+    for i, (buffer, left) in enumerate(((0, BLOCK), (2, 2), (4, 2), (6, BLOCK))):
+        sent = buffers.at[buffer, pl.ds(0, WIDE - left)]
+        arrived(sent, send_sems.at[i])
+
+
+def hand_out(counts, conc, chem, total, conc_out, chem_out, power_out, power_held, sems):
+    copies = [
+        pltpu.make_async_copy(source, target, sems.at[i])
+        for i, (source, target) in enumerate(((conc, conc_out), (chem, chem_out), (power_held, power_out)))
+    ]
+    copies[0].start()
+    copies[1].start()
+    col = lax.axis_index("col")
+    lane_c = lax.broadcasted_iota(jnp.int32, (1, COLS), 1)
+    owned = counts[...]
+    start = jnp.sum(jnp.where(lane_c < col, owned, 0), axis=1, keepdims=True)
+    mine = jnp.sum(jnp.where(lane_c == col, owned, 0), axis=1, keepdims=True)
+    wanted = lax.broadcasted_iota(jnp.int32, (80, LANES), 0) + start
+    lane_1 = lax.broadcasted_iota(jnp.int32, (1, LANES), 1)
+    slot_1 = lax.rem(lane_1, SLOTS)
     found = jnp.zeros((80, LANES), jnp.float32)
     for c in range(COLS):
         for part in range(2):
-            at = c * BLOCK + part * YB
-            values = jnp.broadcast_to(last[at:at + 1, :], (80, LANES))
-            found = found + jnp.where(ids[2 * c + part:2 * c + part + 1, :] == wanted, values, 0.0)
+            values = jnp.broadcast_to(total[2 * c + part:2 * c + part + 1, :], (80, LANES))
+            packed = SPARE * (2 * part + lane_1 // SLOTS) + slot_1 - EVEN
+            plane = jnp.where((slot_1 >= EVEN) & (packed < EVEN), plane_of(c, packed, jnp), -1)
+            found = found + jnp.where(plane == wanted, values, 0.0)
     power = lax.dot_general(
         jnp.ones((8, LANES), jnp.float32), found, (((1,), (1,)), ((), ())),
         precision=lax.Precision.HIGHEST, preferred_element_type=jnp.float32,
     )
     power = jnp.log(power * (1.0 / float(NX * NY * NY * NZ * NZ)) + power_floor)
     power = jnp.where(lax.broadcasted_iota(jnp.int32, (8, 80), 1) < mine, power, 0.0)
-    power_out[...] = power[0:1, :KX_MOST]
-
-    for i, (buffer, left) in enumerate(((0, BLOCK), (2, 2), (4, 2), (6, BLOCK))):
-        sent = buffers.at[buffer, pl.ds(0, WIDE - left)]
-        arrived(sent, send_sems.at[i])
+    power_held[...] = power[0:1, :KX_MOST]
+    copies[2].start()
+    for copy in copies:
+        copy.wait()
 
 
 def shards(concentration, plane_counts):
-    x_table, square, weight, ids = (jnp.asarray(t) for t in tables())
+    table = jnp.asarray(tables())
     vmem = pl.BlockSpec(memory_space=pltpu.VMEM)
-    anywhere = pl.BlockSpec(memory_space=pl.ANY)
-    smem = pl.BlockSpec(memory_space=pltpu.SMEM)
-    conc, chem, power = pl.pallas_call(
-        kernel,
-        out_shape=(
-            jax.ShapeDtypeStruct((YB, 1, NX), jnp.float32),
-            jax.ShapeDtypeStruct((YB, 1, NX), jnp.float32),
-            jax.ShapeDtypeStruct((1, KX_MOST), jnp.float32),
-        ),
-        in_specs=[smem, vmem, anywhere, anywhere, vmem, vmem],
+    hbm = pl.BlockSpec(memory_space=pltpu.HBM)
+    cells = concentration.reshape(YB, 1, NX)
+    field = jax.ShapeDtypeStruct((YB, 1, NX), jnp.float32)
+    held = pl.pallas_call(
+        spectral,
+        out_shape=(field, field, jax.ShapeDtypeStruct((2 * COLS, LANES), jnp.float32)),
+        in_specs=[hbm, hbm],
         out_specs=(vmem, vmem, vmem),
         scratch_shapes=[
-            pltpu.VMEM(x_table.shape, jnp.bfloat16),
-            pltpu.VMEM(square.shape, jnp.bfloat16),
+            pltpu.VMEM(cells.shape, jnp.float32),
+            pltpu.VMEM((2, 2, HALF, X_SHARE), jnp.bfloat16),
+            pltpu.VMEM((2, HALF, X_SHARE), jnp.bfloat16),
             pltpu.VMEM((8, WIDE, LANES), jnp.float32),
-            pltpu.SemaphoreType.DMA((3,)),
             pltpu.SemaphoreType.DMA((4,)),
             pltpu.SemaphoreType.DMA((4,)),
+            pltpu.SemaphoreType.DMA((4,)),
+            pltpu.SemaphoreType.REGULAR,
+            pltpu.SemaphoreType.REGULAR,
+            pltpu.SemaphoreType.REGULAR,
         ],
-        compiler_params=pltpu.CompilerParams(collective_id=0, has_side_effects=True),
-    )(plane_counts, concentration.reshape(YB, 1, NX), x_table, square, weight, ids)
+        compiler_params=pltpu.CompilerParams(
+            collective_id=0, has_side_effects=True, vmem_limit_bytes=VMEM - ROOM
+        ),
+    )(cells, table)
+    conc, chem, power = pl.pallas_call(
+        hand_out,
+        out_shape=(field, field, jax.ShapeDtypeStruct((1, KX_MOST), jnp.float32)),
+        in_specs=[vmem, vmem, vmem, vmem],
+        out_specs=(hbm, hbm, hbm),
+        scratch_shapes=[pltpu.VMEM((1, KX_MOST), jnp.float32), pltpu.SemaphoreType.DMA((3,))],
+        compiler_params=pltpu.CompilerParams(vmem_limit_bytes=4 * 1024 * 1024),
+    )(plane_counts.reshape(1, COLS), *held)
     return conc.reshape(1, YB, NX), chem.reshape(1, YB, NX), power.reshape(KX_MOST)
 
 

time: 58.2 us -> 48.6 us (0.84)
  Pallas kernels: 53.3 us -> 47.8 us
  local copies, waits for them, and re-layouts: 3.98 us -> 0.01 us
    pallas_call x1 -> x2, Pallas kernels: 53.3 us -> 47.8 us  [the longest x1 46.9 us: shards(): pl.pallas_call(spectral, out_shape=(field, field, jax.ShapeDtypeStruct((2...]
    unnamed x3 -> x2, local copies, waits for them, and re-layouts: 3.98 us -> 0.01 us
where the time goes in v2:
time: 48.6 us; the launch traced here: 48.4 us
  Pallas kernels  47.8 us (98%)
  between operations  0.65 us (1%)
    pallas_call x1, Pallas kernels, shards(): pl.pallas_call(spectral, out_shape=(field, field, jax.ShapeDtypeStruct((2...  46.9 us

profile of v2, /device:TPU:1, one launch (start us, length us, event | category | flops | bytes accessed | tf_op | source)
XLA Modules:
  0.0 48.4 jit_solution(15889819033811781731)
XLA Ops:
  0.6 0.0 copy-start
  0.6 46.9 %shard_map.58 = (f32[12,1,768]{2,1,0:T(1,128)S(1)}, f32[12,1,768]{2,1,0:T(1,128)S(1)}, f32[16,128]{1,0:T(8,128)S(1)}) custom-call(f32[12,1,768]{2,1,0:T(1,128)} %bitcast.6, bf16[6,384,512]{2,1,0:T(8,128)(2,1)} %constant.2.clone.tables_hbm), custom_call_target="tpu_custom_call" | custom-call | tf_op jit(solution)/shard_map/pallas_call | solution.py:329
  47.6 0.0 copy-done
  47.6 0.9 %shard_map.59 = (f32[12,1,768]{2,1,0:T(1,128)}, f32[12,1,768]{2,1,0:T(1,128)}, f32[1,73]{1,0:T(1,128)}) custom-call(s32[1,8]{1,0:T(1,128)S(1)} %bitcast.5, f32[12,1,768]{2,1,0:T(1,128)S(1)} %get-tuple-element.9.conc, f32[12,1,768]{2,1,0:T(1,128)S(1)} %get-tuple-element.10.chem, f32[16,128]{1,0:T(8,128)S(1)} %get-tuple-element.11.total), custom_call_target="tpu_custom_call" | custom-call | tf_op jit(solution)/shard_map/pallas_call | solution.py:350
Async XLA Ops:
  0.6 46.9 %copy-start = (s32[8]{0:T(128)S(1)}, s32[8]{0:T(128)}, u32[]{:S(2)}) copy-start(s32[8]{0:T(128)} %param.4) | copy-start | bytes 100

commit v3 on v2

--- a/solution.py
+++ b/solution.py
@@ -15,6 +15,8 @@
 COLS, ROWS = 8, 96
 RING_Z, RING_Y = 12, 8
 FAR_Y = (4, 3, 5, 2, 6, 1, 7)
+START_Y = (0, 1, 2, 3, 7, 6, 5, 4)
+FAR_COL = (4, 5, 3, 2, 6, 7, 1, 0)
 NEAR_Z = (1, 2, 3, -1, -2, -3)
 NEAR_Y = (1, 2, -1, -2)
 YB = NY // COLS
@@ -71,7 +73,7 @@
     z_forward = full.transpose(0, 1, 3, 2).reshape(WIDE, WIDE)
     square = np.zeros((2, HALF, X_SHARE), jnp.bfloat16)
     for k, table in enumerate((y_forward, z_forward, z_forward.T, y_forward.T)):
-        square[:, k // 2 * WIDE:(k // 2 + 1) * WIDE, k % 2 * 256:k % 2 * 256 + WIDE] = split(table)
+        square[k // 2, :, k % 2 * 256:k % 2 * 256 + WIDE] = split(table).reshape(HALF, WIDE)
     return np.concatenate([split(x_table[0]), split(x_table[1]), square])
 
 
@@ -86,29 +88,36 @@
 
 
 def table_times(table, value):
-    high, low = halves(value)
-    inner = ((1,), (0,))
-    return product(table[0], high, inner) + (product(table[1], high, inner) + product(table[0], low, inner))
+    rows, lanes = table.shape[0] // 2, value.shape[1]
+    parts = product(table, jnp.concatenate(halves(value), axis=1), ((1,), (0,)))
+    return parts[:rows, :lanes] + (parts[:rows, lanes:] + parts[rows:, :lanes])
 
 
 def times_table(value, table, contract):
     high, low = halves(value)
-    return product(high, table[0], contract) + (product(low, table[0], contract) + product(high, table[1], contract))
+    rows = value.shape[0]
+    parts = product(jnp.concatenate([high, low]), table[0], contract)
+    return parts[:rows] + (parts[rows:] + product(high, table[1], contract))
 
 
 def signal(semaphore, row, col):
     pl.semaphore_signal(semaphore, inc=1, device_id=(row, col), device_id_type=MESH)
 
 
-def col_exchange(source, target, send, receive, row, col):
+def col_exchange(source, target, send, receive, row, col, peers):
     mine = pl.ds(pl.multiple_of(col * BLOCK, 8), BLOCK)
-    for step in range(1, COLS):
-        peer = lax.rem(col + step, COLS)
+    for peer in peers:
         theirs = pl.ds(pl.multiple_of(peer * BLOCK, 8), BLOCK)
-        pltpu.make_async_remote_copy(
-            source.at[theirs], target.at[mine], send, receive, device_id=(row, peer), device_id_type=MESH
-        ).start()
-    pltpu.make_async_copy(source.at[mine], target.at[mine], receive).start()
+
+        @pl.when(peer != col)
+        def _():
+            pltpu.make_async_remote_copy(
+                source.at[theirs], target.at[mine], send, receive, device_id=(row, peer), device_id_type=MESH
+            ).start()
+
+        @pl.when(peer == col)
+        def _():
+            pltpu.make_async_copy(source.at[mine], target.at[mine], receive).start()
 
 
 def row_exchange(source, target, send, receive, row, col):
@@ -130,6 +139,26 @@
     lax.fori_loop(0, RING_Z - 1, plane, 0)
     for step_y in FAR_Y:
         one(0, step_y)
+    pltpu.make_async_copy(source.at[mine], target.at[mine], receive).start()
+
+
+def row_return(source, target, send, receive, row, col):
+    mine = pl.ds(2 * row, 2)
+
+    def plane(z, carry):
+        for y in START_Y:
+            peer = z * RING_Y + y
+
+            @pl.when(peer != row)
+            def _():
+                pltpu.make_async_remote_copy(
+                    source.at[pl.ds(2 * peer, 2)], target.at[mine], send, receive,
+                    device_id=(peer, col), device_id_type=MESH,
+                ).start()
+
+        return carry
+
+    lax.fori_loop(0, RING_Z, plane, 0)
     pltpu.make_async_copy(source.at[mine], target.at[mine], receive).start()
 
 
@@ -153,13 +182,12 @@
     at_z = [lax.rem(row_z + RING_Z + step, RING_Z) * RING_Y + row_y for step in NEAR_Z]
     at_y = [row_z * RING_Y + lax.rem(row_y + RING_Y + step, RING_Y) for step in NEAR_Y]
     around = [row_z * RING_Y + lax.rem(row_y + step, RING_Y) for step in FAR_Y]
-    loads[0].start()
+    for load in loads:
+        load.start()
     for peer in at_z + at_y:
         signal(barrier, peer, col)
     for step in range(1, COLS):
         signal(barrier, row, lax.rem(col + step, COLS))
-    for load in loads[1:]:
-        load.start()
 
     lane = lax.broadcasted_iota(jnp.int32, (16, LANES), 1)
     first = lane < SLOTS
@@ -180,19 +208,21 @@
             imag = jnp.where(first, pltpu.roll(top, SLOTS, 1), bottom)
             out[base:base + YB, :] = real[:YB]
             out[base + YB:base + BLOCK, :] = imag[:YB]
-
-    pl.semaphore_wait(barrier, len(at_z) + len(at_y) + COLS - 1)
-    col_exchange(buffers.at[0], buffers.at[1], send_sems.at[0], recv_sems.at[0], row, col)
-    for peer in at_z:
-        signal(near_z, peer, col)
-    for peer in at_y:
-        signal(near_y, peer, col)
+        if parity == 0:
+            pl.semaphore_wait(barrier, len(at_z) + len(at_y) + COLS - 1)
+            for peer in at_z:
+                signal(near_z, peer, col)
+            for peer in at_y:
+                signal(near_y, peer, col)
+        half = COLS // 2
+        peers = [parity * half + lax.rem(col + step, half) for step in (2, 1, 3, 0)]
+        col_exchange(buffers.at[0], buffers.at[1], send_sems.at[0], recv_sems.at[0], row, col, peers)
+
     loads[3].wait()
 
 
     def middle(k):
-        rows, lanes = pl.ds(k // 2 * WIDE, WIDE), pl.ds(k % 2 * 256, WIDE)
-        return square[0, rows, lanes], square[1, rows, lanes]
+        return square[k // 2, :, pl.ds(k % 2 * 256, WIDE)]
 
     lane_w = lax.broadcasted_iota(jnp.int32, (NZ, LANES), 1)
     kz = lax.broadcasted_iota(jnp.int32, (NZ, LANES), 0)
@@ -234,7 +264,7 @@
     )
     field = table_times(middle(2), jnp.concatenate([real, imag])).reshape(WIDE // 8, 8, LANES)
     buffers[4] = jnp.where(spare_8[None], packed[None], field).reshape(WIDE, LANES)
-    row_exchange(buffers.at[4], buffers.at[5], send_sems.at[2], recv_sems.at[2], row, col)
+    row_return(buffers.at[4], buffers.at[5], send_sems.at[2], recv_sems.at[2], row, col)
     arrived(buffers.at[5], recv_sems.at[2])
     gathered = buffers[5]
     total = jnp.sum(gathered.reshape(WIDE // 8, 8, LANES), axis=0)
@@ -248,7 +278,8 @@
     spare_b = lax.rem(lane_b, SLOTS) >= EVEN
     field = table_times(middle(3), gathered).reshape(COLS, BLOCK, LANES)
     buffers[6] = jnp.where(spare_b[None], totals[None], field).reshape(WIDE, LANES)
-    col_exchange(buffers.at[6], buffers.at[7], send_sems.at[3], recv_sems.at[3], row, col)
+    col_exchange(buffers.at[6], buffers.at[7], send_sems.at[3], recv_sems.at[3], row, col,
+        [lax.rem(col + step, COLS) for step in FAR_COL])
 
     lane_1 = lax.broadcasted_iota(jnp.int32, (1, LANES), 1)
     slot_1 = lax.rem(lane_1, SLOTS)

time: 48.6 us -> 47.7 us (0.981)
  Pallas kernels: 47.8 us -> 46.8 us
    pallas_call x1, Pallas kernels: 46.9 us -> 46 us  [shards(): pl.pallas_call(spectral, out_shape=(field, field, jax.ShapeDtypeStruct((2...]
where the time goes in v3:
time: 47.7 us; the launch traced here: 47.5 us
  Pallas kernels  46.8 us (98%)
  between operations  0.65 us (1%)
    pallas_call x1, Pallas kernels, shards(): pl.pallas_call(spectral, out_shape=(field, field, jax.ShapeDtypeStruct((2...  46 us

profile of v3, /device:TPU:1, one launch (start us, length us, event | category | flops | bytes accessed | tf_op | source)
XLA Modules:
  0.0 47.5 jit_solution(8265383386907306569)
XLA Ops:
  0.6 0.0 copy-start
  0.6 46.0 %shard_map.58 = (f32[12,1,768]{2,1,0:T(1,128)S(1)}, f32[12,1,768]{2,1,0:T(1,128)S(1)}, f32[16,128]{1,0:T(8,128)S(1)}) custom-call(f32[12,1,768]{2,1,0:T(1,128)} %bitcast.6, bf16[6,384,512]{2,1,0:T(8,128)(2,1)} %constant.2.clone.tables_hbm), custom_call_target="tpu_custom_call" | custom-call | tf_op jit(solution)/shard_map/pallas_call | solution.py:360
  46.6 0.0 copy-done
  46.6 0.9 %shard_map.59 = (f32[12,1,768]{2,1,0:T(1,128)}, f32[12,1,768]{2,1,0:T(1,128)}, f32[1,73]{1,0:T(1,128)}) custom-call(s32[1,8]{1,0:T(1,128)S(1)} %bitcast.5, f32[12,1,768]{2,1,0:T(1,128)S(1)} %get-tuple-element.9.conc, f32[12,1,768]{2,1,0:T(1,128)S(1)} %get-tuple-element.10.chem, f32[16,128]{1,0:T(8,128)S(1)} %get-tuple-element.11.total), custom_call_target="tpu_custom_call" | custom-call | tf_op jit(solution)/shard_map/pallas_call | solution.py:381
Async XLA Ops:
  0.6 46.0 %copy-start = (s32[8]{0:T(128)S(1)}, s32[8]{0:T(128)}, u32[]{:S(2)}) copy-start(s32[8]{0:T(128)} %param.4) | copy-start | bytes 100

commit v4 on v3

--- a/solution.py
+++ b/solution.py
@@ -15,6 +15,7 @@
 COLS, ROWS = 8, 96
 RING_Z, RING_Y = 12, 8
 FAR_Y = (4, 3, 5, 2, 6, 1, 7)
+FAR_Z = (6, 5, 7, 4, 8, 3, 9, 2, 10, 1, 11)
 START_Y = (0, 1, 2, 3, 7, 6, 5, 4)
 FAR_COL = (4, 5, 3, 2, 6, 7, 1, 0)
 NEAR_Z = (1, 2, 3, -1, -2, -3)
@@ -120,26 +121,32 @@
             pltpu.make_async_copy(source.at[mine], target.at[mine], receive).start()
 
 
-def row_exchange(source, target, send, receive, row, col):
+def row_exchange(source, target, send, receive, row, col, ring_y):
     mine = pl.ds(2 * row, 2)
     row_z, row_y = row // RING_Y, lax.rem(row, RING_Y)
-
-    def one(step_z, step_y):
-        peer = lax.rem(row_z + step_z, RING_Z) * RING_Y + lax.rem(row_y + step_y, RING_Y)
+    far_z = [lax.rem(row_z + step, RING_Z) * RING_Y for step in FAR_Z]
+
+    def one(peer):
         pltpu.make_async_remote_copy(
             source.at[pl.ds(2 * peer, 2)], target.at[mine], send, receive, device_id=(peer, col), device_id_type=MESH
         ).start()
 
-    def plane(i, carry):
-        step_z = RING_Z // 2 + (1 - 2 * lax.rem(i, 2)) * ((i + 1) // 2)
-        for step_y in FAR_Y + (0,):
-            one(step_z, step_y)
+    def column(i, carry):
+        y = i + i // 4 * (11 - 2 * i)
+
+        @pl.when(y != row_y)
+        def _():
+            pl.semaphore_wait(ring_y.at[y], 1)
+            for first in far_z:
+                one(first + y)
+            one(row_z * RING_Y + y)
+
         return carry
 
-    lax.fori_loop(0, RING_Z - 1, plane, 0)
-    for step_y in FAR_Y:
-        one(0, step_y)
+    for first in far_z:
+        one(first + row_y)
     pltpu.make_async_copy(source.at[mine], target.at[mine], receive).start()
+    lax.fori_loop(0, RING_Y, column, 0)
 
 
 def row_return(source, target, send, receive, row, col):
@@ -182,12 +189,18 @@
     at_z = [lax.rem(row_z + RING_Z + step, RING_Z) * RING_Y + row_y for step in NEAR_Z]
     at_y = [row_z * RING_Y + lax.rem(row_y + RING_Y + step, RING_Y) for step in NEAR_Y]
     around = [row_z * RING_Y + lax.rem(row_y + step, RING_Y) for step in FAR_Y]
-    for load in loads:
-        load.start()
     for peer in at_z + at_y:
         signal(barrier, peer, col)
     for step in range(1, COLS):
         signal(barrier, row, lax.rem(col + step, COLS))
+    for load in loads:
+        load.start()
+
+    pl.semaphore_wait(barrier, len(at_z) + len(at_y) + COLS - 1)
+    for peer in at_z:
+        signal(near_z, peer, col)
+    for peer in at_y:
+        signal(near_y, peer, col)
 
     lane = lax.broadcasted_iota(jnp.int32, (16, LANES), 1)
     first = lane < SLOTS
@@ -208,16 +221,14 @@
             imag = jnp.where(first, pltpu.roll(top, SLOTS, 1), bottom)
             out[base:base + YB, :] = real[:YB]
             out[base + YB:base + BLOCK, :] = imag[:YB]
-        if parity == 0:
-            pl.semaphore_wait(barrier, len(at_z) + len(at_y) + COLS - 1)
-            for peer in at_z:
-                signal(near_z, peer, col)
-            for peer in at_y:
-                signal(near_y, peer, col)
         half = COLS // 2
         peers = [parity * half + lax.rem(col + step, half) for step in (2, 1, 3, 0)]
         col_exchange(buffers.at[0], buffers.at[1], send_sems.at[0], recv_sems.at[0], row, col, peers)
 
+    pl.semaphore_wait(near_z, len(at_z))
+    pl.semaphore_wait(near_y, len(at_y))
+    for peer in around:
+        signal(ring_y.at[row_y], peer, col)
     loads[3].wait()
 
 
@@ -236,14 +247,9 @@
     damping = 1.0 / (1.0 + time_step * grad_coeff * squared * squared)
     mixing = jnp.where(lane_w < SLOTS, -time_step * squared, grad_coeff * squared)
 
-    pl.semaphore_wait(near_z, len(at_z))
-    pl.semaphore_wait(near_y, len(at_y))
-    for peer in around:
-        signal(ring_y, peer, col)
     arrived(buffers.at[1], recv_sems.at[0])
     buffers[2] = table_times(middle(0), buffers[1])
-    pl.semaphore_wait(ring_y, len(around))
-    row_exchange(buffers.at[2], buffers.at[3], send_sems.at[1], recv_sems.at[1], row, col)
+    row_exchange(buffers.at[2], buffers.at[3], send_sems.at[1], recv_sems.at[1], row, col, ring_y)
     arrived(buffers.at[3], recv_sems.at[1])
     hat = table_times(middle(1), buffers[3])
     real, imag = hat[:NZ], hat[NZ:]
@@ -278,15 +284,15 @@
     spare_b = lax.rem(lane_b, SLOTS) >= EVEN
     field = table_times(middle(3), gathered).reshape(COLS, BLOCK, LANES)
     buffers[6] = jnp.where(spare_b[None], totals[None], field).reshape(WIDE, LANES)
-    col_exchange(buffers.at[6], buffers.at[7], send_sems.at[3], recv_sems.at[3], row, col,
+    col_exchange(buffers.at[6], buffers.at[7], send_sems.at[3], recv_sems.at[3 + col // (COLS // 2)], row, col,
         [lax.rem(col + step, COLS) for step in FAR_COL])
 
     lane_1 = lax.broadcasted_iota(jnp.int32, (1, LANES), 1)
     slot_1 = lax.rem(lane_1, SLOTS)
     last = buffers.at[7]
-    arrived(last, recv_sems.at[3])
     sums = []
     for parity in range(2):
+        arrived(buffers.at[7, pl.ds(parity * (WIDE // 2), WIDE // 2)], recv_sems.at[3 + parity])
         pieces = []
         for j in range(COLS // 2):
             c = parity * (COLS // 2) + j
@@ -369,10 +375,10 @@
             pltpu.VMEM((8, WIDE, LANES), jnp.float32),
             pltpu.SemaphoreType.DMA((4,)),
             pltpu.SemaphoreType.DMA((4,)),
-            pltpu.SemaphoreType.DMA((4,)),
+            pltpu.SemaphoreType.DMA((5,)),
             pltpu.SemaphoreType.REGULAR,
             pltpu.SemaphoreType.REGULAR,
-            pltpu.SemaphoreType.REGULAR,
+            pltpu.SemaphoreType.REGULAR((RING_Y,)),
         ],
         compiler_params=pltpu.CompilerParams(
             collective_id=0, has_side_effects=True, vmem_limit_bytes=VMEM - ROOM

time: 47.7 us -> 47.4 us (level)
  no operation moved by 1% of the time
where the time goes in v4:
time: 47.4 us; the launch traced here: 47.3 us
  Pallas kernels  46.6 us (98%)
  between operations  0.65 us (1%)
    pallas_call x1, Pallas kernels, shards(): pl.pallas_call(spectral, out_shape=(field, field, jax.ShapeDtypeStruct((2...  45.8 us

profile of v4, /device:TPU:1, one launch (start us, length us, event | category | flops | bytes accessed | tf_op | source)
XLA Modules:
  0.0 47.3 jit_solution(17636652417249692016)
XLA Ops:
  0.6 0.0 copy-start
  0.6 45.8 %shard_map.58 = (f32[12,1,768]{2,1,0:T(1,128)S(1)}, f32[12,1,768]{2,1,0:T(1,128)S(1)}, f32[16,128]{1,0:T(8,128)S(1)}) custom-call(f32[12,1,768]{2,1,0:T(1,128)} %bitcast.6, bf16[6,384,512]{2,1,0:T(8,128)(2,1)} %constant.2.clone.tables_hbm), custom_call_target="tpu_custom_call" | custom-call | tf_op jit(solution)/shard_map/pallas_call | solution.py:366
  46.4 0.0 copy-done
  46.4 0.9 %shard_map.59 = (f32[12,1,768]{2,1,0:T(1,128)}, f32[12,1,768]{2,1,0:T(1,128)}, f32[1,73]{1,0:T(1,128)}) custom-call(s32[1,8]{1,0:T(1,128)S(1)} %bitcast.5, f32[12,1,768]{2,1,0:T(1,128)S(1)} %get-tuple-element.9.conc, f32[12,1,768]{2,1,0:T(1,128)S(1)} %get-tuple-element.10.chem, f32[16,128]{1,0:T(8,128)S(1)} %get-tuple-element.11.total), custom_call_target="tpu_custom_call" | custom-call | tf_op jit(solution)/shard_map/pallas_call | solution.py:387
Async XLA Ops:
  0.6 45.8 %copy-start = (s32[8]{0:T(128)S(1)}, s32[8]{0:T(128)}, u32[]{:S(2)}) copy-start(s32[8]{0:T(128)} %param.4) | copy-start | bytes 100
